TPU v7x, 32 devices: a whole 2x2x4 slice. The times are simulated.
32 devices in a mesh: expert: 8 (over z, y), mp: 4 (over x, core).
Axes of the slice: x: 2, y: 2, z: 4, core: 2. Of those that a mesh axis runs over, the one named last changes fastest.
Arguments:
- tokens: bfloat16 [1024, 3584], P('expert', 'mp'), may hold values from -6 to 6
- assignments: int32 [1024, 2], P('expert'), may hold values from 0 to 7, all different within a row; in each aligned block of 128 rows (0 to 127, 128 to 255, ...) at most 64 rows name the same one
- gate_probs: float32 [1024, 2], P('expert'), may hold values from 0.05 to 0.5
- expert_gate: bfloat16 [8, 3584, 2560], P('expert', None, 'mp'), may hold values from -0.09375 to 0.09375
- expert_up: bfloat16 [8, 3584, 2560], P('expert', None, 'mp'), may hold values from -0.09375 to 0.09375
- expert_down: bfloat16 [8, 2560, 3584], P('expert', 'mp'), may hold values from -0.125 to 0.125
- shared_gate: bfloat16 [3584, 10240], P('mp', 'expert'), may hold values from -0.09375 to 0.09375
- shared_up: bfloat16 [3584, 10240], P('mp', 'expert'), may hold values from -0.09375 to 0.09375
- shared_down_weight: bfloat16 [10240, 3584], P('expert', 'mp'), may hold values from -0.0625 to 0.0625
Outputs:
- layer_out: bfloat16 [1024, 3584], P('expert', 'mp')
Inputs may be any that keep to these rules, and one draw needn't show every extreme that they name: `assignments`: each row names 2 different experts; among the 128 rows of one index of the expert axis (aligned blocks) no expert is named more than 64 times.
All inputs are finite; a program needn't handle non-finite values.
Results may differ from a plain program's by a relative error of at most 0.0075.
Values may be sent and summed in bfloat16 or wider, within the bound.
No kernel may reach another device: no remote copies, remote signals or barrier semaphores. Data moves between devices by JAX's collectives and lax.ppermute only.
A program may use at most 128 MiB of HBM per device.

v0:
```python
import jax
import jax.numpy as jnp
from jax import lax
from jax.sharding import PartitionSpec as P


def split_parts(values):
    high = values.astype(jnp.bfloat16)
    low = (values - high.astype(jnp.float32)).astype(jnp.bfloat16)
    return (high, low)


def on_device(
    tokens,
    assignments,
    gate_probs,
    expert_gate,
    expert_up,
    expert_down,
    shared_gate,
    shared_up,
    shared_down_weight,
):
    experts = lax.axis_size("expert")
    local_rows, chosen = assignments.shape
    capacity = min(local_rows, max(2, 2 * local_rows * chosen // experts))
    slots_all = experts * capacity
    shared_hidden_width = shared_gate.shape[1]
    joined = jnp.concatenate([shared_gate, shared_up], axis=1)
    shared_both = jnp.dot(
        lax.all_gather(tokens, "expert", axis=0, tiled=True),
        joined,
        preferred_element_type=jnp.float32,
    )
    share = lax.psum_scatter(shared_both, "mp", scatter_dimension=0, tiled=True)
    hidden_portion_part = (
        jax.nn.silu(share[:, :shared_hidden_width]) * share[:, shared_hidden_width:]
    ).astype(jnp.bfloat16)
    shared_hidden = lax.all_gather(hidden_portion_part, "mp", axis=0, tiled=True)
    shared_result = lax.psum_scatter(
        jnp.dot(shared_hidden, shared_down_weight, preferred_element_type=jnp.float32),
        "expert",
        scatter_dimension=0,
        tiled=True,
    )
    flat_ids = assignments.reshape(-1)
    pairs = flat_ids.shape[0]
    onehot = (jnp.arange(experts, dtype=jnp.int32)[:, None] == flat_ids[None, :]).astype(jnp.int32)
    slot_rank = jnp.sum((jnp.cumsum(onehot, axis=1) - onehot) * onehot, axis=0)
    column = flat_ids * capacity + slot_rank
    picker = (column[:, None] == jnp.arange(slots_all, dtype=jnp.int32)[None, :]).astype(
        jnp.float32
    )
    owner_row = jnp.arange(pairs, dtype=jnp.int32) // chosen
    folding = (jnp.arange(local_rows, dtype=jnp.int32)[:, None] == owner_row[None, :]).astype(
        jnp.float32
    )
    indicator = jnp.dot(folding, picker, precision=lax.Precision.HIGHEST)
    dispatch = indicator.T.astype(jnp.bfloat16)
    combine = jnp.dot(
        folding, picker * gate_probs.reshape(-1)[:, None], precision=lax.Precision.HIGHEST
    )
    combine_high, combine_low = split_parts(combine)
    weight_gate = expert_gate[0]
    weight_up = expert_up[0]
    weight_down = expert_down[0]
    outgoing = jnp.dot(dispatch, tokens, preferred_element_type=jnp.float32).astype(jnp.bfloat16)
    received = lax.all_to_all(
        outgoing.reshape(experts, capacity, -1), "expert", split_axis=0, concat_axis=0, tiled=True
    )
    received = received.reshape(slots_all, -1)
    portion = lax.all_gather(received, "mp", axis=1, tiled=True)
    gate_acc = jnp.dot(portion, weight_gate, preferred_element_type=jnp.float32)
    up_acc = jnp.dot(portion, weight_up, preferred_element_type=jnp.float32)
    hidden = (jax.nn.silu(gate_acc) * up_acc).astype(jnp.bfloat16)
    partial_value = jnp.dot(hidden, weight_down, preferred_element_type=jnp.float32).astype(
        jnp.bfloat16
    )
    returned = lax.all_to_all(
        partial_value.reshape(experts, capacity, -1),
        "expert",
        split_axis=0,
        concat_axis=0,
        tiled=True,
    )
    returned = returned.reshape(slots_all, -1)
    local_sum = jnp.dot(combine_high, returned, preferred_element_type=jnp.float32) + jnp.dot(
        combine_low, returned, preferred_element_type=jnp.float32
    )
    routed = lax.psum_scatter(local_sum, "mp", scatter_dimension=1, tiled=True)
    return (shared_result + routed).astype(jnp.bfloat16)


def solution(mesh):
    in_specs = (
        P("expert", "mp"),
        P("expert", None),
        P("expert", None),
        P("expert", None, "mp"),
        P("expert", None, "mp"),
        P("expert", "mp", None),
        P("mp", "expert"),
        P("mp", "expert"),
        P("expert", "mp"),
    )
    out_specs = P("expert", "mp")
    return jax.shard_map(
        on_device, mesh=mesh, in_specs=in_specs, out_specs=out_specs, check_vma=False
    )
```

profile of v0, /device:TPU:0, one launch (start us, length us, event | category | flops | bytes accessed | tf_op | source)
XLA Modules:
  0.0 340.1 jit_solution(3035032161229359272)
XLA Ops:
  6.5 0.0 copy-start
  6.5 0.0 all-gather.4.cloned.1.call-start
  6.5 0.7 all-gather.4.cloned.1.call-update
  7.3 0.0 all-gather.8.cloned.1.call-start
  7.3 0.8 copy.11
  8.1 0.7 broadcast_multiply_fusion
  8.8 0.1 copy.10
  8.9 0.1 mul.44
  9.0 0.1 eq.53
  9.2 0.6 reduce-window.6
  9.8 0.2 slice_reduce_fusion
  10.0 0.1 select_reduce_fusion
  10.1 0.4 convolution_convert_fusion.2
  10.5 1.3 convolution_convert_fusion.1
  11.8 38.0 %all_to_all.10 = bf16[8,64,896]{2,1,0:T(8,128)(2,1)} all-to-all(bf16[8,64,896]{2,1,0:T(8,128)(2,1)S(1)} %bitcast.33), channel_id=1, replica_groups=mesh['expert'=8,'mp'=4] {'expert'}, dimensions={0} | all-to-all | bytes 1835008 | tf_op jit(solution)/shard_map/all_to_all | solution.py:68
  49.8 0.0 all-gather.8.cloned.1.call-update
  49.8 0.0 reduce-scatter.4.cloned.1.call-start
  49.9 17.3 %all-gather.4.cloned.1.call-done = bf16[1024,896]{1,0:T(8,128)(2,1)} async-done(((bf16[128,896]{1,0:T(8,128)(2,1)}), bf16[1024,896]{1,0:T(8,128)(2,1)}) %all-gather.4.cloned.1.call-update) | async-done | bytes 1835024 | tf_op jit(solution)/shard_map/all_gather | solution.py:31
  67.2 11.0 %convolution_bitcast_fusion = f32[1024,2560]{0,1:T(8,128)} fusion(bf16[1024,896]{1,0:T(8,128)(2,1)} %all-gather.4.cloned.1.call-done, bf16[896,1280]{1,0:T(8,128)(2,1)} %param.16, bf16[896,1280]{1,0:T(8,128)(2,1)} %param.15), kind=kOutput, calls=%fused_computation | convolution fusion | flops 4706795520 | bytes 16908288 | tf_op jit(solution)/shard_map/dot_general | solution.py:30
  78.2 0.0 reduce-scatter.4.cloned.1.call-update
  78.2 20.7 %all-gather.8.cloned.1.call-done = bf16[512,3584]{1,0:T(8,128)(2,1)} async-done(((bf16[512,896]{1,0:T(8,128)(2,1)}), bf16[512,3584]{1,0:T(8,128)(2,1)}) %all-gather.8.cloned.1.call-update) | async-done | bytes 3670032 | tf_op jit(solution)/shard_map/all_gather | solution.py:72
  99.0 0.0 copy-start.2
  99.0 6.5 %fusion.6 = f32[512,640]{1,0:T(8,128)S(1)} fusion(bf16[512,3584]{1,0:T(8,128)(2,1)} %all-gather.8.cloned.1.call-done, bf16[1,3584,640]{2,1,0:T(8,128)(2,1)} %param.12), kind=kOutput, calls=%fused_computation.9 | convolution fusion | flops 2348810240 | bytes 9568256 | tf_op jit(solution)/shard_map/dot_general | solution.py:73
  105.5 0.0 copy-done.2
  105.5 6.2 %fusion.11 = bf16[512,640]{1,0:T(8,128)(2,1)S(1)} fusion(bf16[512,3584]{1,0:T(8,128)(2,1)S(1)} %copy-done.2, bf16[1,3584,640]{2,1,0:T(8,128)(2,1)} %param.13, f32[512,640]{1,0:T(8,128)S(1)} %fusion.6), kind=kOutput, calls=%fused_computation.13 | convolution fusion | flops 2350776320 | bytes 10223616 | tf_op jit(solution)/shard_map/dot_general | solution.py:74
  111.7 8.3 %convolution_convert_fusion = bf16[512,3584]{1,0:T(8,128)(2,1)} fusion(bf16[512,640]{1,0:T(8,128)(2,1)S(1)} %fusion.11, bf16[1,640,3584]{2,1,0:T(8,128)(2,1)} %param.14), kind=kOutput, calls=%fused_computation.1 | convolution fusion | flops 2350645248 | bytes 8912896 | tf_op jit(solution)/shard_map/dot_general | solution.py:76
  120.0 5.2 %all-to-all-start.1 = ((bf16[8,64,3584]{2,1,0:T(8,128)(2,1)}), bf16[8,64,3584]{2,1,0:T(8,128)(2,1)}, u32[]{:S(2)}, u32[]{:S(2)}) async-start(bf16[8,64,3584]{2,1,0:T(8,128)(2,1)} %bitcast.31), calls=%async_computation.3 | async-start | bytes 7340032 | tf_op jit(solution)/shard_map/all_to_all | solution.py:79
  125.2 0.0 copy-start.1
  125.2 0.0 all-gather.6.cloned.1.call-start
  125.3 60.5 %reduce-scatter.4.cloned.1.call-done = f32[256,2560]{0,1:T(8,128)} async-done(((f32[1024,2560]{0,1:T(8,128)}), f32[256,2560]{0,1:T(8,128)}) %reduce-scatter.4.cloned.1.call-update) | async-done | bytes 2621456 | tf_op jit(solution)/shard_map/reduce_scatter | solution.py:35
  185.8 3.0 fusion.14
  188.8 0.0 all-gather.6.cloned.1.call-update
  188.8 0.2 reduce-scatter.8.cloned.1.call-start
  189.0 0.0 copy-done.1
  189.0 0.1 copy.12
  189.2 0.1 mul.46
  189.3 0.5 fusion.15
  189.8 18.0 %all-to-all-done.1 = bf16[8,64,3584]{2,1,0:T(8,128)(2,1)} async-done(((bf16[8,64,3584]{2,1,0:T(8,128)(2,1)}), bf16[8,64,3584]{2,1,0:T(8,128)(2,1)}, u32[]{:S(2)}, u32[]{:S(2)}) %all-to-all-start.1) | async-done | bytes 3670048 | tf_op jit(solution)/shard_map/all_to_all | solution.py:79
  207.8 2.7 fusion.24
  210.5 4.0 %convolution_add_fusion = f32[128,3584]{1,0:T(8,128)} fusion(f32[128,3584]{1,0:T(8,128)S(1)} %fusion.24, bf16[512,3584]{1,0:T(8,128)(2,1)} %bitcast.8, f32[128,512]{1,0:T(8,128)S(1)} %fusion.15), kind=kOutput, calls=%fused_computation.2 | convolution fusion | flops 470482944 | bytes 7602176 | tf_op jit(solution)/shard_map/dot_general | solution.py:87
  214.5 0.0 reduce-scatter.8.cloned.1.call-update
  214.5 0.0 reduce-scatter.6.cloned.1.call-start
  214.6 0.3 all-gather.6.cloned.1.call-done
  214.9 0.0 copy-done
  214.9 6.5 %fusion.31 = f32[1024,896]{1,0:T(8,128)} fusion(bf16[1024,1280]{0,1:T(8,128)(2,1)} %all-gather.6.cloned.1.call-done, bf16[1280,896]{1,0:T(8,128)(2,1)S(1)} %copy-done), kind=kOutput, calls=%fused_computation.45 | convolution fusion | flops 2348810240 | bytes 8585216 | tf_op jit(solution)/shard_map/dot_general | solution.py:41
  221.3 0.0 reduce-scatter.6.cloned.1.call-update
  221.3 25.5 %reduce-scatter.8.cloned.1.call-done = f32[128,896]{1,0:T(8,128)} async-done(((f32[128,3584]{1,0:T(8,128)}), f32[128,896]{1,0:T(8,128)}) %reduce-scatter.8.cloned.1.call-update) | async-done | bytes 458768 | tf_op jit(solution)/shard_map/reduce_scatter | solution.py:90
  246.9 84.5 %reduce-scatter.6.cloned.1.call-done = f32[128,896]{1,0:T(8,128)} async-done(((f32[1024,896]{1,0:T(8,128)}), f32[128,896]{1,0:T(8,128)}) %reduce-scatter.6.cloned.1.call-update) | async-done | bytes 458768 | tf_op jit(solution)/shard_map/reduce_scatter | solution.py:40
  331.3 1.9 add_convert_fusion
  (4 shorter events, 0.1 us)
Async XLA Ops:
  6.5 208.3 %copy-start = (bf16[1280,896]{1,0:T(8,128)(2,1)S(1)}, bf16[1280,896]{1,0:T(8,128)(2,1)}, u32[]{:S(2)}) copy-start(bf16[1280,896]{1,0:T(8,128)(2,1)} %param.17) | copy-start | bytes 6881284
  6.5 60.7 %all-gather.4.cloned.1.call-start = ((), (), s32[]{:S(2)}) async-start(), calls=%async_computation.5 | async-start | bytes 2064384 | tf_op jit(solution)/shard_map/all_gather | solution.py:31
  7.3 91.7 %all-gather.8.cloned.1.call-start = ((), (), s32[]{:S(2)}) async-start(), calls=%async_computation.9 | async-start | bytes 4587520 | tf_op jit(solution)/shard_map/all_gather | solution.py:72
  49.8 136.0 %reduce-scatter.4.cloned.1.call-start = ((), (), s32[]{:S(2)}) async-start(), calls=%async_computation.6 | async-start | bytes 13107200 | tf_op jit(solution)/shard_map/reduce_scatter | solution.py:35
  99.0 6.6 %copy-start.2 = (bf16[512,3584]{1,0:T(8,128)(2,1)S(1)}, bf16[512,3584]{1,0:T(8,128)(2,1)}, u32[]{:S(2)}) copy-start(bf16[512,3584]{1,0:T(8,128)(2,1)} %all-gather.8.cloned.1.call-done) | copy-start | bytes 11010052
  120.0 87.8 %all-to-all-start.1 = ((bf16[8,64,3584]{2,1,0:T(8,128)(2,1)}), bf16[8,64,3584]{2,1,0:T(8,128)(2,1)}, u32[]{:S(2)}, u32[]{:S(2)}) async-start(bf16[8,64,3584]{2,1,0:T(8,128)(2,1)} %bitcast.31), calls=%async_computation.3 | async-start | bytes 7340032 | tf_op jit(solution)/shard_map/all_to_all | solution.py:79
  125.2 63.8 %copy-start.1 = (f32[128,2]{0,1:T(2,128)S(1)}, f32[128,2]{0,1:T(2,128)}, u32[]{:S(2)}) copy-start(f32[128,2]{0,1:T(2,128)} %param.11) | copy-start | bytes 3076
  125.2 89.6 %all-gather.6.cloned.1.call-start = ((), (), s32[]{:S(2)}) async-start(), calls=%async_computation.7 | async-start | bytes 3276800 | tf_op jit(solution)/shard_map/all_gather | solution.py:39
  188.8 58.1 %reduce-scatter.8.cloned.1.call-start = ((), (), s32[]{:S(2)}) async-start(), calls=%async_computation.10 | async-start | bytes 2293760 | tf_op jit(solution)/shard_map/reduce_scatter | solution.py:90
  214.5 116.8 %reduce-scatter.6.cloned.1.call-start = ((), (), s32[]{:S(2)}) async-start(), calls=%async_computation.8 | async-start | bytes 4128768 | tf_op jit(solution)/shard_map/reduce_scatter | solution.py:40
Sparse Core Ops, SparseCore 0:
  9.5 57.6 all-gather.3
  68.8 30.1 all-gather.7
  101.6 84.1 reduce-scatter.3
  188.9 25.8 all-gather.5
  217.2 29.5 reduce-scatter.7
  250.4 80.9 reduce-scatter.5
where the time goes:
time: 341 us; the launch traced here: 340 us
  waiting for transfers between devices  228 us (67%)
  matrix products  47.3 us (14%)
  blocking collectives  38 us (11%)
  between operations  13.6 us (4%)
  other arithmetic  6.28 us (2%)
  starting transfers between devices  5.61 us (2%)
    reduce_scatter x1, waiting for transfers between devices, on_device(): lax.psum_scatter(jnp.dot(shared_hidden, shared_down_weight, preferred_ele...  84.5 us
    reduce_scatter x1, waiting for transfers between devices, on_device(): share = lax.psum_scatter(shared_both, 'mp', scatter_dimension=0, tiled=True)  60.5 us
    all_to_all x1, blocking collectives, on_device(): lax.all_to_all(outgoing.reshape(experts, capacity, -1), 'expert', split_a...  38 us
    reduce_scatter x1, waiting for transfers between devices, on_device(): routed = lax.psum_scatter(local_sum, 'mp', scatter_dimension=1, tiled=True)  25.5 us
    all_gather x1, waiting for transfers between devices, on_device(): portion = lax.all_gather(received, 'mp', axis=1, tiled=True)  20.7 us
    all_to_all x1, waiting for transfers between devices, on_device(): lax.all_to_all(partial_value.reshape(experts, capacity, -1), 'expert', sp...  18 us
    all_gather x1, waiting for transfers between devices, on_device(): lax.all_gather(tokens, 'expert', axis=0, tiled=True)  17.3 us
    dot_general x1, matrix products, on_device(): jnp.dot(lax.all_gather(tokens, 'expert', axis=0, tiled=True), joined, pre...  11 us
  transfers between devices with their start and end apart: 7, of which 7 were waited for; matrix products, arithmetic and copies ran while one was open for 16% of the time, Pallas kernels for 0%

commit v1 on v0

--- a/solution.py
+++ b/solution.py
@@ -2,6 +2,17 @@
 import jax.numpy as jnp
 from jax import lax
 from jax.sharding import PartitionSpec as P
+
+
+def cut_along(x, dim, devices):
+    before, after = (x.shape[:dim], x.shape[dim + 1 :])
+    return jnp.moveaxis(x.reshape(*before, devices, -1, *after), dim, 0)
+
+
+def laid_out(pieces, dim):
+    pieces = jnp.moveaxis(pieces, 0, dim)
+    lengths = pieces.shape
+    return pieces.reshape(*lengths[:dim], lengths[dim] * lengths[dim + 1], *lengths[dim + 2 :])
 
 
 def split_parts(values):
@@ -65,9 +76,16 @@
     weight_up = expert_up[0]
     weight_down = expert_down[0]
     outgoing = jnp.dot(dispatch, tokens, preferred_element_type=jnp.float32).astype(jnp.bfloat16)
-    received = lax.all_to_all(
-        outgoing.reshape(experts, capacity, -1), "expert", split_axis=0, concat_axis=0, tiled=True
-    )
+    x = outgoing.reshape(experts, capacity, -1)
+    size, mine = (lax.axis_size("expert"), lax.axis_index("expert"))
+    blocks = cut_along(x, 0, size)
+    filled = blocks
+    for step in range(1, size):
+        target, source = ((mine + step) % size, (mine - step) % size)
+        sent = lax.dynamic_index_in_dim(blocks, target, 0)
+        other = lax.ppermute(sent, "expert", [(i, (i + step) % size) for i in range(size)])
+        filled = lax.dynamic_update_slice_in_dim(filled, other, source, axis=0)
+    received = laid_out(filled, 0)
     received = received.reshape(slots_all, -1)
     portion = lax.all_gather(received, "mp", axis=1, tiled=True)
     gate_acc = jnp.dot(portion, weight_gate, preferred_element_type=jnp.float32)

time: 341 us -> 343 us (level)
  blocking collectives: 38 us -> 0 us
  waiting for transfers between devices: 228 us -> 258 us
  starting transfers between devices: 5.61 us -> 16.7 us
  matrix products: 47.3 us -> 43.8 us
    all_to_all x1 -> x0, blocking collectives: 38 us -> none  [on_device(): lax.all_to_all(outgoing.reshape(experts, capacity, -1), 'expert', split_a...]
    ppermute x0 -> x7, waiting for transfers between devices: none -> 20.1 us  [on_device(): lax.ppermute(sent, 'expert', [(i, (i + step) % size) for i in range(size)])]
    ppermute x0 -> x7, starting transfers between devices: none -> 11 us  [on_device(): lax.ppermute(sent, 'expert', [(i, (i + step) % size) for i in range(size)])]
    all_gather x1, waiting for transfers between devices: 17.3 us -> 24.6 us  [on_device(): lax.all_gather(tokens, 'expert', axis=0, tiled=True)]
    dot_general x1, matrix products: 8.27 us -> 4.82 us  [on_device(): jnp.dot(hidden, weight_down, preferred_element_type=jnp.float32)]
  transfers between devices with their start and end apart: 7 -> 14, of which waited for: 7 -> 11; matrix products, arithmetic and copies ran while one was open for 16% -> 15% of each run, Pallas kernels for 0% -> 0%
where the time goes in v1:
time: 343 us
  waiting for transfers between devices  258 us (75%)
  matrix products  43.8 us (13%)
  starting transfers between devices  16.7 us (5%)
  between operations  13.7 us (4%)
  other arithmetic  6.26 us (2%)
  local copies, waits for them, and re-layouts  4.1 us (1%)
    reduce_scatter x1, waiting for transfers between devices, on_device(): lax.psum_scatter(jnp.dot(shared_hidden, shared_down_weight, preferred_ele...  84.4 us
    reduce_scatter x1, waiting for transfers between devices, on_device(): share = lax.psum_scatter(shared_both, 'mp', scatter_dimension=0, tiled=True)  63.8 us
    reduce_scatter x1, waiting for transfers between devices, on_device(): routed = lax.psum_scatter(local_sum, 'mp', scatter_dimension=1, tiled=True)  25.5 us
    all_gather x1, waiting for transfers between devices, on_device(): lax.all_gather(tokens, 'expert', axis=0, tiled=True)  24.6 us
    all_gather x1, waiting for transfers between devices, on_device(): portion = lax.all_gather(received, 'mp', axis=1, tiled=True)  20.8 us
    ppermute x7, waiting for transfers between devices, on_device(): lax.ppermute(sent, 'expert', [(i, (i + step) % size) for i in range(size)])  20.1 us
    all_to_all x1, waiting for transfers between devices, on_device(): lax.all_to_all(partial_value.reshape(experts, capacity, -1), 'expert', sp...  14.7 us
    ppermute x7, starting transfers between devices, on_device(): lax.ppermute(sent, 'expert', [(i, (i + step) % size) for i in range(size)])  11 us
  transfers between devices with their start and end apart: 14, of which 11 were waited for; matrix products, arithmetic and copies ran while one was open for 15% of the time, Pallas kernels for 0%

profile of v1, /device:TPU:0, one launch (start us, length us, event | category | flops | bytes accessed | tf_op | source)
XLA Modules:
  0.0 342.8 jit_solution(18373507152985194445)
XLA Ops:
  6.5 0.0 copy-start
  6.5 0.0 all-gather.4.cloned.1.call-start
  6.5 0.7 all-gather.4.cloned.1.call-update
  7.3 0.0 all-gather.8.cloned.1.call-start
  7.3 0.8 copy.11
  8.1 0.7 broadcast_multiply_fusion
  8.8 0.1 copy.10
  8.9 0.1 mul.44
  9.0 0.1 eq.68
  9.2 0.6 reduce-window.6
  9.8 0.2 slice_reduce_fusion
  10.0 0.1 select_reduce_fusion
  10.2 0.0 copy-start.3
  10.2 0.0 copy-start.5
  10.2 0.6 copy-done.3
  10.7 0.0 copy-done.5
  10.7 0.4 convolution_convert_fusion.2
  11.1 1.3 convolution_convert_fusion.1
  12.5 3.1 collective-permute-start
  15.5 6.2 %collective-permute-done = bf16[1,1,64,896]{3,2,0,1:T(8,128)(2,1)S(1)} collective-permute-done((bf16[1,1,64,896]{3,2,0,1:T(8,128)(2,1)S(1)}, bf16[1,1,64,896]{3,2,0,1:T(8,128)(2,1)S(1)}, u32[]{:S(2)}, u32[]{:S(2)}) %collective-permute-start) | collective-permute-done | bytes 114720 | tf_op jit(solution)/shard_map/ppermute | solution.py:86
  21.7 0.8 constant_dynamic-slice_fusion
  22.5 0.0 collective-permute-start.1
  22.5 1.3 collective-permute-start.2
  23.8 1.2 collective-permute-start.3
  25.0 3.5 %collective-permute-start.4 = (bf16[1,1,64,896]{3,2,0,1:T(8,128)(2,1)}, bf16[1,1,64,896]{3,2,0,1:T(8,128)(2,1)S(1)}, u32[]{:S(2)}, u32[]{:S(2)}) collective-permute-start(bf16[1,1,64,896]{3,2,0,1:T(8,128)(2,1)} %get-tuple-element.7), channel_id=1, source_target_pairs={{0,20},{4,24},{8,28},{12,0},{16,4},{20,8},{24,12},{28,16},{1,21},{... | collective-permute-start | bytes 344072 | tf_op jit(solution)/shard_map/ppermute | solution.py:86
  28.5 1.6 collective-permute-start.5
  30.1 2.3 collective-permute-done.1
  32.5 0.3 collective-permute-start.6
  32.8 8.1 %collective-permute-done.2 = bf16[1,1,64,896]{3,2,0,1:T(8,128)(2,1)S(1)} collective-permute-done((bf16[1,1,64,896]{3,2,0,1:T(8,128)(2,1)}, bf16[1,1,64,896]{3,2,0,1:T(8,128)(2,1)S(1)}, u32[]{:S(2)}, u32[]{:S(2)}) %collective-permute-start.2) | collective-permute-done | bytes 114720 | tf_op jit(solution)/shard_map/ppermute | solution.py:86
  40.9 3.4 %collective-permute-done.3 = bf16[1,1,64,896]{3,2,0,1:T(8,128)(2,1)S(1)} collective-permute-done((bf16[1,1,64,896]{3,2,0,1:T(8,128)(2,1)}, bf16[1,1,64,896]{3,2,0,1:T(8,128)(2,1)S(1)}, u32[]{:S(2)}, u32[]{:S(2)}) %collective-permute-start.3) | collective-permute-done | bytes 114720 | tf_op jit(solution)/shard_map/ppermute | solution.py:86
  44.4 0.0 collective-permute-done.4
  44.4 0.0 collective-permute-done.5
  44.4 0.0 collective-permute-done.6
  44.5 0.9 copy-done.1
  45.4 0.0 all-gather.8.cloned.1.call-update
  45.4 0.0 reduce-scatter.4.cloned.1.call-start
  45.5 24.6 %all-gather.4.cloned.1.call-done = bf16[1024,896]{1,0:T(8,128)(2,1)} async-done(((bf16[128,896]{1,0:T(8,128)(2,1)}), bf16[1024,896]{1,0:T(8,128)(2,1)}) %all-gather.4.cloned.1.call-update) | async-done | bytes 1835024 | tf_op jit(solution)/shard_map/all_gather | solution.py:42
  70.0 10.9 %convolution_bitcast_fusion = f32[1024,2560]{0,1:T(8,128)} fusion(bf16[1024,896]{1,0:T(8,128)(2,1)} %all-gather.4.cloned.1.call-done, bf16[896,1280]{1,0:T(8,128)(2,1)} %param.16, bf16[896,1280]{1,0:T(8,128)(2,1)} %param.15), kind=kOutput, calls=%fused_computation | convolution fusion | flops 4706795520 | bytes 16908288 | tf_op jit(solution)/shard_map/dot_general | solution.py:41
  81.0 0.0 reduce-scatter.4.cloned.1.call-update
  81.0 20.8 %all-gather.8.cloned.1.call-done = bf16[512,3584]{1,0:T(8,128)(2,1)} async-done(((bf16[512,896]{1,0:T(8,128)(2,1)}), bf16[512,3584]{1,0:T(8,128)(2,1)}) %all-gather.8.cloned.1.call-update) | async-done | bytes 3670032 | tf_op jit(solution)/shard_map/all_gather | solution.py:90
  101.8 6.5 %fusion.4 = f32[512,640]{1,0:T(8,128)S(1)} fusion(bf16[512,3584]{1,0:T(8,128)(2,1)} %all-gather.8.cloned.1.call-done, bf16[1,3584,640]{2,1,0:T(8,128)(2,1)} %param.13), kind=kOutput, calls=%fused_computation.7 | convolution fusion | flops 2348810240 | bytes 9568256 | tf_op jit(solution)/shard_map/dot_general | solution.py:92
  108.4 0.0 slice-start.1
  108.4 6.2 %fusion.6 = f32[512,640]{1,0:T(8,128)S(1)} fusion(bf16[512,3584]{1,0:T(8,128)(2,1)S(1)} %copy-done.7, bf16[1,3584,640]{2,1,0:T(8,128)(2,1)} %param.12), kind=kOutput, calls=%fused_computation.9 | convolution fusion | flops 2348810240 | bytes 9568256 | tf_op jit(solution)/shard_map/dot_general | solution.py:91
  114.6 4.8 %convolution_convert_fusion = bf16[512,3584]{1,0:T(8,128)(2,1)} fusion(bf16[1,640,3584]{2,1,0:T(8,128)(2,1)S(1)} %bitcast.31, f32[512,640]{1,0:T(8,128)S(1)} %fusion.4, f32[512,640]{1,0:T(8,128)S(1)} %fusion.6), kind=kOutput, calls=%fused_computation.1 | convolution fusion | flops 2352611328 | bytes 10878976 | tf_op jit(solution)/shard_map/dot_general | solution.py:94
  119.5 5.3 %all-to-all-start = ((bf16[8,64,3584]{2,1,0:T(8,128)(2,1)}), bf16[8,64,3584]{2,1,0:T(8,128)(2,1)}, u32[]{:S(2)}, u32[]{:S(2)}) async-start(bf16[8,64,3584]{2,1,0:T(8,128)(2,1)} %bitcast.29), calls=%async_computation.2 | async-start | bytes 7340032 | tf_op jit(solution)/shard_map/all_to_all | solution.py:97
  124.8 0.0 all-gather.6.cloned.1.call-start
  124.8 63.8 %reduce-scatter.4.cloned.1.call-done = f32[256,2560]{0,1:T(8,128)} async-done(((f32[1024,2560]{0,1:T(8,128)}), f32[256,2560]{0,1:T(8,128)}) %reduce-scatter.4.cloned.1.call-update) | async-done | bytes 2621456 | tf_op jit(solution)/shard_map/reduce_scatter | solution.py:46
  188.7 3.0 fusion.8
  191.6 0.0 all-gather.6.cloned.1.call-update
  191.6 0.2 reduce-scatter.8.cloned.1.call-start
  191.9 0.1 copy.12
  192.0 0.1 mul.46
  192.2 0.4 fusion.10
  192.6 14.7 %all-to-all-done = bf16[8,64,3584]{2,1,0:T(8,128)(2,1)} async-done(((bf16[8,64,3584]{2,1,0:T(8,128)(2,1)}), bf16[8,64,3584]{2,1,0:T(8,128)(2,1)}, u32[]{:S(2)}, u32[]{:S(2)}) %all-to-all-start) | async-done | bytes 3670048 | tf_op jit(solution)/shard_map/all_to_all | solution.py:97
  207.3 2.7 fusion.19
  210.0 4.0 %convolution_add_fusion = f32[128,3584]{1,0:T(8,128)} fusion(f32[128,3584]{1,0:T(8,128)S(1)} %fusion.19, bf16[512,3584]{1,0:T(8,128)(2,1)} %bitcast.8, f32[128,512]{1,0:T(8,128)S(1)} %fusion.10), kind=kOutput, calls=%fused_computation.2 | convolution fusion | flops 470482944 | bytes 7602176 | tf_op jit(solution)/shard_map/dot_general | solution.py:105
  214.0 0.0 reduce-scatter.8.cloned.1.call-update
  214.0 0.0 reduce-scatter.6.cloned.1.call-start
  214.1 3.6 %all-gather.6.cloned.1.call-done = bf16[1024,1280]{0,1:T(8,128)(2,1)} async-done(((bf16[256,1280]{0,1:T(8,128)(2,1)}), bf16[1024,1280]{0,1:T(8,128)(2,1)}) %all-gather.6.cloned.1.call-update) | async-done | bytes 2621456 | tf_op jit(solution)/shard_map/all_gather | solution.py:50
  217.7 6.4 %fusion.27 = f32[1024,896]{1,0:T(8,128)} fusion(bf16[1024,1280]{0,1:T(8,128)(2,1)} %all-gather.6.cloned.1.call-done, bf16[1280,896]{1,0:T(8,128)(2,1)S(1)} %copy-done), kind=kOutput, calls=%fused_computation.60 | convolution fusion | flops 2348810240 | bytes 8585216 | tf_op jit(solution)/shard_map/dot_general | solution.py:52
  224.1 0.0 reduce-scatter.6.cloned.1.call-update
  224.1 25.5 %reduce-scatter.8.cloned.1.call-done = f32[128,896]{1,0:T(8,128)} async-done(((f32[128,3584]{1,0:T(8,128)}), f32[128,896]{1,0:T(8,128)}) %reduce-scatter.8.cloned.1.call-update) | async-done | bytes 458768 | tf_op jit(solution)/shard_map/reduce_scatter | solution.py:108
  249.7 84.4 %reduce-scatter.6.cloned.1.call-done = f32[128,896]{1,0:T(8,128)} async-done(((f32[1024,896]{1,0:T(8,128)}), f32[128,896]{1,0:T(8,128)}) %reduce-scatter.6.cloned.1.call-update) | async-done | bytes 458768 | tf_op jit(solution)/shard_map/reduce_scatter | solution.py:51
  334.1 1.9 add_convert_fusion
  (25 shorter events, 0.2 us)
Async XLA Ops:
  6.5 211.1 %copy-start = (bf16[1280,896]{1,0:T(8,128)(2,1)S(1)}, bf16[1280,896]{1,0:T(8,128)(2,1)}, u32[]{:S(2)}) copy-start(bf16[1280,896]{1,0:T(8,128)(2,1)} %param.17) | copy-start | bytes 6881284
  6.5 63.5 %all-gather.4.cloned.1.call-start = ((), (), s32[]{:S(2)}) async-start(), calls=%async_computation.4 | async-start | bytes 2064384 | tf_op jit(solution)/shard_map/all_gather | solution.py:42
  7.3 94.6 %all-gather.8.cloned.1.call-start = ((), (), s32[]{:S(2)}) async-start(), calls=%async_computation.8 | async-start | bytes 4587520 | tf_op jit(solution)/shard_map/all_gather | solution.py:90
  10.2 0.6 copy-start.3
  10.2 0.6 copy-start.5
  12.5 9.2 %collective-permute-start = (bf16[1,1,64,896]{3,2,0,1:T(8,128)(2,1)S(1)}, bf16[1,1,64,896]{3,2,0,1:T(8,128)(2,1)S(1)}, u32[]{:S(2)}, u32[]{:S(2)}) collective-permute-start(bf16[1,1,64,896]{3,2,0,1:T(8,128)(2,1)S(1)} %constant_dynamic-slice_fusion.6), channel_id=1, source_target_pairs={{0,4},{4,8},{8,12},{12,16},{16,20},{20,24},{24,28},{28,0},{1,5},{5... | collective-permute-start | bytes 344072 | tf_op jit(solution)/shard_map/ppermute | solution.py:86
  22.5 10.0 %collective-permute-start.1 = (bf16[1,1,64,896]{3,2,0,1:T(8,128)(2,1)}, bf16[1,1,64,896]{3,2,0,1:T(8,128)(2,1)S(1)}, u32[]{:S(2)}, u32[]{:S(2)}) collective-permute-start(bf16[1,1,64,896]{3,2,0,1:T(8,128)(2,1)} %get-tuple-element.10), channel_id=1, source_target_pairs={{0,8},{4,12},{8,16},{12,20},{16,24},{20,28},{24,0},{28,4},{1,9},{5... | collective-permute-start | bytes 344072 | tf_op jit(solution)/shard_map/ppermute | solution.py:86
  22.5 18.4 %collective-permute-start.2 = (bf16[1,1,64,896]{3,2,0,1:T(8,128)(2,1)}, bf16[1,1,64,896]{3,2,0,1:T(8,128)(2,1)S(1)}, u32[]{:S(2)}, u32[]{:S(2)}) collective-permute-start(bf16[1,1,64,896]{3,2,0,1:T(8,128)(2,1)} %get-tuple-element.9), channel_id=1, source_target_pairs={{0,12},{4,16},{8,20},{12,24},{16,28},{20,0},{24,4},{28,8},{1,13},{... | collective-permute-start | bytes 344072 | tf_op jit(solution)/shard_map/ppermute | solution.py:86
  23.8 20.6 %collective-permute-start.3 = (bf16[1,1,64,896]{3,2,0,1:T(8,128)(2,1)}, bf16[1,1,64,896]{3,2,0,1:T(8,128)(2,1)S(1)}, u32[]{:S(2)}, u32[]{:S(2)}) collective-permute-start(bf16[1,1,64,896]{3,2,0,1:T(8,128)(2,1)} %get-tuple-element.8), channel_id=1, source_target_pairs={{0,16},{4,20},{8,24},{12,28},{16,0},{20,4},{24,8},{28,12},{1,17},{... | collective-permute-start | bytes 344072 | tf_op jit(solution)/shard_map/ppermute | solution.py:86
  25.0 19.4 %collective-permute-start.4 = (bf16[1,1,64,896]{3,2,0,1:T(8,128)(2,1)}, bf16[1,1,64,896]{3,2,0,1:T(8,128)(2,1)S(1)}, u32[]{:S(2)}, u32[]{:S(2)}) collective-permute-start(bf16[1,1,64,896]{3,2,0,1:T(8,128)(2,1)} %get-tuple-element.7), channel_id=1, source_target_pairs={{0,20},{4,24},{8,28},{12,0},{16,4},{20,8},{24,12},{28,16},{1,21},{... | collective-permute-start | bytes 344072 | tf_op jit(solution)/shard_map/ppermute | solution.py:86
  28.5 15.8 %collective-permute-start.5 = (bf16[1,1,64,896]{3,2,0,1:T(8,128)(2,1)S(1)}, bf16[1,1,64,896]{3,2,0,1:T(8,128)(2,1)S(1)}, u32[]{:S(2)}, u32[]{:S(2)}) collective-permute-start(bf16[1,1,64,896]{3,2,0,1:T(8,128)(2,1)S(1)} %get-tuple-element.6), channel_id=1, source_target_pairs={{0,24},{4,28},{8,0},{12,4},{16,8},{20,12},{24,16},{28,20},{1,25},{... | collective-permute-start | bytes 344072 | tf_op jit(solution)/shard_map/ppermute | solution.py:86
  32.5 12.0 %collective-permute-start.6 = (bf16[1,1,64,896]{3,2,0,1:T(8,128)(2,1)S(1)}, bf16[1,1,64,896]{3,2,0,1:T(8,128)(2,1)S(1)}, u32[]{:S(2)}, u32[]{:S(2)}) collective-permute-start(bf16[1,1,64,896]{3,2,0,1:T(8,128)(2,1)S(1)} %get-tuple-element.5), channel_id=1, source_target_pairs={{0,28},{4,0},{8,4},{12,8},{16,12},{20,16},{24,20},{28,24},{1,29},{... | collective-permute-start | bytes 344072 | tf_op jit(solution)/shard_map/ppermute | solution.py:86
  44.5 0.9 copy-start.1
  45.4 143.2 %reduce-scatter.4.cloned.1.call-start = ((), (), s32[]{:S(2)}) async-start(), calls=%async_computation.5 | async-start | bytes 13107200 | tf_op jit(solution)/shard_map/reduce_scatter | solution.py:46
  101.8 6.6 %copy-start.7 = (bf16[512,3584]{1,0:T(8,128)(2,1)S(1)}, bf16[512,3584]{1,0:T(8,128)(2,1)}, u32[]{:S(2)}) copy-start(bf16[512,3584]{1,0:T(8,128)(2,1)} %all-gather.8.cloned.1.call-done) | copy-start | bytes 11010052
  101.8 12.8 %slice-start = ((s8[4587520]{0:T(1024)(128)(4,1)}), s8[4194304]{0:T(1024)(128)(4,1)S(1)}, s32[]{:S(2)}) async-start(s8[4587520]{0:T(1024)(128)(4,1)} %bitcast.30), calls=%async_computation.10 | async-start | bytes 8388608
  108.4 6.2 %slice-start.1 = ((s8[4587520]{0:T(1024)(128)(4,1)}), s8[393216]{0:T(1024)(128)(4,1)S(1)}, s32[]{:S(2)}) async-start(s8[4587520]{0:T(1024)(128)(4,1)} %bitcast.30), calls=%async_computation.11 | async-start | bytes 786432
  119.5 87.9 %all-to-all-start = ((bf16[8,64,3584]{2,1,0:T(8,128)(2,1)}), bf16[8,64,3584]{2,1,0:T(8,128)(2,1)}, u32[]{:S(2)}, u32[]{:S(2)}) async-start(bf16[8,64,3584]{2,1,0:T(8,128)(2,1)} %bitcast.29), calls=%async_computation.2 | async-start | bytes 7340032 | tf_op jit(solution)/shard_map/all_to_all | solution.py:97
  124.8 67.1 %copy-start.2 = (f32[128,2]{0,1:T(2,128)S(1)}, f32[128,2]{0,1:T(2,128)}, u32[]{:S(2)}) copy-start(f32[128,2]{0,1:T(2,128)} %param.11) | copy-start | bytes 3076
  124.8 67.4 %copy-start.4 = (s32[256]{0:T(256)S(1)}, s32[256]{0:T(256)}, u32[]{:S(2)}) copy-start(s32[256]{0:T(256)} %copy-done.3) | copy-start | bytes 3076
  124.8 67.4 %copy-start.6 = (s32[256]{0:T(256)S(1)}, s32[256]{0:T(256)}, u32[]{:S(2)}) copy-start(s32[256]{0:T(256)} %copy-done.5) | copy-start | bytes 3076
  124.8 92.9 %all-gather.6.cloned.1.call-start = ((), (), s32[]{:S(2)}) async-start(), calls=%async_computation.6 | async-start | bytes 3276800 | tf_op jit(solution)/shard_map/all_gather | solution.py:50
  191.6 58.0 %reduce-scatter.8.cloned.1.call-start = ((), (), s32[]{:S(2)}) async-start(), calls=%async_computation.9 | async-start | bytes 2293760 | tf_op jit(solution)/shard_map/reduce_scatter | solution.py:108
  214.0 120.0 %reduce-scatter.6.cloned.1.call-start = ((), (), s32[]{:S(2)}) async-start(), calls=%async_computation.7 | async-start | bytes 4128768 | tf_op jit(solution)/shard_map/reduce_scatter | solution.py:51
Sparse Core Ops, SparseCore 0:
  9.5 60.4 all-gather.3
  71.6 30.1 all-gather.7
  104.4 84.1 reduce-scatter.3
  191.8 25.8 all-gather.5
  220.0 29.5 reduce-scatter.7
  253.2 80.8 reduce-scatter.5
